TPU v7x, 32 devices: a whole 2x2x4 slice. The times are simulated.
32 devices in a mesh: groups: 2 (over y), ctx: 4 (over z), tp: 4 (over x, core).
Axes of the slice: x: 2, y: 2, z: 4, core: 2. Of those that a mesh axis runs over, the one named last changes fastest.
Arguments:
- prompt_q: bfloat16 [1536, 8192], P(('groups', 'ctx'), 'tp'), parts along dimension 0, may hold values from -12 to 12
- prompt_k: bfloat16 [1536, 1024], P(('groups', 'ctx'), 'tp'), parts along dimension 0, may hold values from -12 to 12
- prompt_v: bfloat16 [1536, 1024], P(('groups', 'ctx'), 'tp'), parts along dimension 0, may hold values from -6 to 6
- stretch_offset: int32 [2], P('groups'), parts along dimension 0, may hold values from 0 to 32767
- step_q: bfloat16 [32, 4, 8192], P(('groups', 'ctx'), None, 'tp'), parts along dimension 0, may hold values from -12 to 12
- step_k: bfloat16 [32, 4, 1024], P(('groups', 'ctx'), None, 'tp'), parts along dimension 0, may hold values from -12 to 12
- step_v: bfloat16 [32, 4, 1024], P(('groups', 'ctx'), None, 'tp'), parts along dimension 0, may hold values from -6 to 6
- cache_len: int32 [32], P('groups'), parts along dimension 0, may hold values from 1 to 768, as said below
- slot_row: int32 [32], P('groups'), parts along dimension 0, may hold values from 0 to 15, each once
- out_weight: bfloat16 [8192, 8192], P('tp', 'ctx'), may hold values from -0.0625 to 0.0625
Outputs:
- prompt_out: bfloat16 [1536, 8192], P(('groups', 'ctx'), 'tp'), parts along dimension 0
- prompt_keys: bfloat16 [1536, 1024], P(('groups', 'ctx'), 'tp'), parts along dimension 0
- step_out: bfloat16 [32, 4, 8192], P('groups', None, ('ctx', 'tp')), parts along dimension 0
There are 2 independent parts, one for each index of `groups`. A program takes and returns all parts, laid end to end along the dimension named above; an argument that names none is the same for every part. Nothing has to cross between parts.
Inputs may be any that keep to these rules, and one draw needn't show every extreme that they name: cache_len[r] counts the first tokens of the prompt stretch that row r's cache holds; some row holds all 768. `slot_row`: each row stands in exactly one slot.
All inputs are finite; a program needn't handle non-finite values.
Results may differ from a plain program's by a relative error of at most 0.015.
Values may be sent and summed in bfloat16 or wider, within the bound.
No kernel may reach another device: no remote copies, remote signals or barrier semaphores. Data moves between devices by JAX's collectives and lax.ppermute only.
A program may use at most 64 MiB of HBM per device.

v0:
```python
import math

import jax
import jax.numpy as jnp
from jax import lax
from jax.sharding import PartitionSpec as P

HQ = 64
KVH = 8
HD = 128


rope_base = 500000.0
floor_score = -1e30


def rotate(values, positions):
    heads = values.shape[-1] // HD
    half = HD // 2
    shaped = values.reshape(values.shape[:-1] + (heads, HD)).astype(jnp.float32)
    freqs = jnp.exp(jnp.arange(half, dtype=jnp.float32) * (-2.0 * math.log(rope_base) / HD))
    angles = positions.astype(jnp.float32)[..., None, None] * freqs
    cosine = jnp.cos(angles)
    sine = jnp.sin(angles)
    first = shaped[..., :half]
    second = shaped[..., half:]
    turned = jnp.concatenate(
        [first * cosine - second * sine, second * cosine + first * sine], axis=-1
    )
    return turned.reshape(values.shape).astype(jnp.bfloat16)


def fold_scores(state, scores, allowed, values, form):
    maxima, totals, weighted = state
    scores = jnp.where(allowed, scores, floor_score)
    newest = jnp.maximum(maxima, scores.max(-1))
    decay = jnp.exp(maxima - newest)
    probs = jnp.where(allowed, jnp.exp(scores - newest[..., None]), 0.0)
    totals = totals * decay + probs.sum(-1)
    weighted = weighted * decay[..., None] + jnp.einsum(
        form, probs.astype(jnp.bfloat16), values, preferred_element_type=jnp.float32
    )
    return (newest, totals, weighted)


def blank_state(leading):
    return (
        jnp.full(leading, floor_score, jnp.float32),
        jnp.zeros(leading, jnp.float32),
        jnp.zeros(leading + (HD,), jnp.float32),
    )


def decode_slots(
    step_query, step_keys, step_values, lengths, cache_keys, cache_values, kv_local, group, scale
):
    slot_rows = step_query.shape[0]
    steps = step_query.shape[1]
    query_slots = step_query.reshape(slot_rows, steps, kv_local, group, HD)
    own_keys = step_keys.reshape(slot_rows, steps, kv_local, HD)
    own_values = step_values.reshape(slot_rows, steps, kv_local, HD)
    own_scores = (
        jnp.einsum("rthgd,ruhd->rhgtu", query_slots, own_keys, preferred_element_type=jnp.float32)
        * scale
    )
    causal = jnp.arange(steps)[None, :] <= jnp.arange(steps)[:, None]
    state = fold_scores(
        blank_state((slot_rows, kv_local, group, steps)),
        own_scores,
        causal,
        own_values,
        "rhgtu,ruhd->rhgtd",
    )
    total_rows = cache_keys.shape[0]
    span = 512 if total_rows % 512 == 0 else total_rows
    keys_heads = cache_keys.reshape(total_rows, kv_local, HD)
    values_heads = cache_values.reshape(total_rows, kv_local, HD)
    needed = (jnp.max(lengths) + span - 1) // span

    def visit_block(position, current):
        key_start = (position * span).astype(jnp.int32)
        keys = lax.dynamic_slice_in_dim(keys_heads, key_start, span, 0)
        values = lax.dynamic_slice_in_dim(values_heads, key_start, span, 0)
        scores = (
            jnp.einsum("rthgd,khd->rhgtk", query_slots, keys, preferred_element_type=jnp.float32)
            * scale
        )
        allowed = (key_start + jnp.arange(span, dtype=jnp.int32))[None, :] < lengths[:, None]
        return fold_scores(
            current, scores, allowed[:, None, None, None, :], values, "rhgtk,khd->rhgtd"
        )

    state = lax.fori_loop(0, needed, visit_block, state)
    attended = (state[2] / state[1][..., None]).astype(jnp.bfloat16)
    return attended.transpose(0, 3, 1, 2, 4).reshape(slot_rows, steps, kv_local * group * HD)


def local(
    prompt_q,
    prompt_k,
    prompt_v,
    stretch_offset,
    step_q,
    step_k,
    step_v,
    cache_len,
    slot_row,
    out_weight,
):
    group = HQ // KVH
    scale = HD ** (-0.5)
    local_rows = prompt_q.shape[0]
    kv_local = prompt_k.shape[1] // HD
    ctx_index = lax.axis_index("ctx")
    query_start = ctx_index * local_rows
    offset = stretch_offset[0]
    prompt_pos = offset + query_start + jnp.arange(local_rows, dtype=jnp.int32)
    prompt_query = rotate(prompt_q, prompt_pos).reshape(local_rows, kv_local, group, HD)
    prompt_keys = rotate(prompt_k, prompt_pos)
    query_pos = query_start + jnp.arange(local_rows, dtype=jnp.int32)

    def attend_unit(state, keys, values, key_start):
        scores = (
            jnp.einsum("qhgd,khd->hgqk", prompt_query, keys, preferred_element_type=jnp.float32)
            * scale
        )
        key_pos = key_start + jnp.arange(keys.shape[0], dtype=jnp.int32)
        allowed = key_pos[None, :] <= query_pos[:, None]
        return fold_scores(state, scores, allowed, values, "hgqk,khd->hgqd")

    initial = blank_state((kv_local, group, local_rows))
    state = initial
    keys_all = lax.all_gather(prompt_keys, "ctx", axis=0, tiled=True).reshape(-1, kv_local, HD)
    values_all = lax.all_gather(prompt_v, "ctx", axis=0, tiled=True).reshape(-1, kv_local, HD)
    count = keys_all.shape[0]
    shards = max(1, 1024 // local_rows)
    while shards > 1 and count % (shards * local_rows) != 0:
        shards -= 1
    unit = shards * local_rows
    turns = count // unit
    keys_units = keys_all.reshape(turns, unit, kv_local, HD)
    values_units = values_all.reshape(turns, unit, kv_local, HD)

    def one_unit(carry, item):
        keys, values, position = item
        key_start = position * unit
        carry = lax.cond(
            key_start <= query_start + local_rows - 1,
            lambda current: attend_unit(current, keys, values, key_start),
            lambda current: current,
            carry,
        )
        return (carry, None)

    state, ignored = lax.scan(
        one_unit, state, (keys_units, values_units, jnp.arange(turns, dtype=jnp.int32))
    )
    cache_keys, cache_values = (
        lax.all_gather(prompt_keys, "ctx", axis=0, tiled=True),
        lax.all_gather(prompt_v, "ctx", axis=0, tiled=True),
    )
    prompt_out = (state[2] / state[1][..., None]).astype(jnp.bfloat16)
    prompt_out = prompt_out.transpose(2, 0, 1, 3).reshape(local_rows, kv_local * group * HD)
    slot_rows = step_q.shape[0]
    steps = step_q.shape[1]
    batch_rows = cache_len.shape[0]
    matches = slot_row[:, None] == jnp.arange(batch_rows, dtype=jnp.int32)[None, :]
    all_lengths = jnp.sum(jnp.where(matches, cache_len[None, :], 0), axis=1)
    my_lengths = lax.dynamic_slice_in_dim(all_lengths, ctx_index * slot_rows, slot_rows, 0)
    step_pos = offset + my_lengths[:, None] + jnp.arange(steps, dtype=jnp.int32)[None, :]
    step_query = rotate(step_q, step_pos)
    step_keys = rotate(step_k, step_pos)
    attended = decode_slots(
        step_query, step_keys, step_v, my_lengths, cache_keys, cache_values, kv_local, group, scale
    )
    columns = jnp.einsum(
        "rte,ef->rtf",
        lax.all_gather(attended, "ctx", axis=0, tiled=True),
        out_weight,
        preferred_element_type=jnp.float32,
    )
    step_out = lax.psum_scatter(columns.astype(jnp.bfloat16), "tp", scatter_dimension=2, tiled=True)
    return (prompt_out, prompt_keys, step_out)


def solution(mesh):
    in_specs = (
        P(("groups", "ctx"), "tp"),
        P(("groups", "ctx"), "tp"),
        P(("groups", "ctx"), "tp"),
        P("groups"),
        P(("groups", "ctx"), None, "tp"),
        P(("groups", "ctx"), None, "tp"),
        P(("groups", "ctx"), None, "tp"),
        P("groups"),
        P("groups"),
        P("tp", "ctx"),
    )
    out_specs = (
        P(("groups", "ctx"), "tp"),
        P(("groups", "ctx"), "tp"),
        P("groups", None, ("ctx", "tp")),
    )
    return jax.shard_map(local, mesh=mesh, in_specs=in_specs, out_specs=out_specs, check_vma=False)
```

profile of v0, /device:TPU:0, one launch (start us, length us, event | category | flops | bytes accessed | tf_op | source)
XLA Modules:
  0.0 98.9 jit_solution(16452795346125733154)
XLA Ops:
  7.2 0.0 reduce-scatter.2.cloned.1.call-start
  7.3 0.9 select_reduce_fusion
  8.1 0.7 fusion.49
  10.2 0.1 add_convert_fusion.3
  10.2 0.7 bitcast_convert_fusion
  10.9 0.9 reshape.203
  11.8 0.1 multiply_cosine_fusion.1
  12.0 0.1 subtract_convert_fusion.2
  12.1 0.1 subtract_convert_fusion.1
  12.2 0.1 maximum_bitcast_fusion
  12.3 0.5 fusion.51
  12.8 0.1 fusion.38
  12.9 0.3 convolution_add_fusion
  13.3 0.4 multiply_cosine_fusion
  13.7 1.0 %reshape.201 = f32[192,2,128]{2,1,0:T(2,128)S(1)} reshape(bf16[192,256]{1,0:T(8,128)(2,1)} %param.15) | data formatting | bytes 294912 | tf_op jit(solution)/shard_map/convert_element_type | solution.py:20
  14.7 0.5 subtract_convert_fusion
  15.1 0.3 pad_maximum_fusion.1
  15.4 0.6 copy-done.2
  16.1 16.3 %all_gather.11 = bf16[768,256]{1,0:T(8,128)(2,1)S(1)} all-gather(bf16[192,256]{1,0:T(8,128)(2,1)S(1)} %bitcast.137), channel_id=1, replica_groups=mesh['groups'=2,'ctx'=4,'tp'=4] {'ctx'}, dimensions={0}, use_global_device_ids=true | all-gather | bytes 491520 | tf_op jit(solution)/shard_map/all_gather | solution.py:133
  32.4 15.5 %all_gather.12 = bf16[768,256]{1,0:T(8,128)(2,1)S(1)} all-gather(bf16[192,256]{1,0:T(8,128)(2,1)S(1)} %copy-done.5), channel_id=1, replica_groups=mesh['groups'=2,'ctx'=4,'tp'=4] {'ctx'}, dimensions={0}, use_global_device_ids=true | all-gather | bytes 491520 | tf_op jit(solution)/shard_map/all_gather | solution.py:134
  47.9 0.2 copy.54
  48.1 0.2 copy.66
  48.3 1.2 %while.2 = (s32[]{:T(128)}, f32[4,2,8,4]{2,3,0,1:T(4,128)S(1)}, f32[4,2,8,4]{2,3,0,1:T(4,128)S(1)}, f32[4,2,8,4,128]{4,2,3,0,1:T(8,128)S(1)}, s32[]{:T(128)}, /*...) while((s32[]{:T(128)}, f32[4,2,8,4]{2,3,0,1:T(4,128)S(1)}, ...), condition=%wide.region_11.12_spmd, body=%wide.region_8.11_spmd.sunk | while | flops 102502656 | bytes 3508365 | solution.py:93
  48.4 0.1 broadcast_compare_fusion.2
  48.4 0.4 fusion.64
  48.8 0.3 fusion.65
  49.1 0.4 fusion.66
  49.5 0.1 fusion.36
  49.7 14.1 %all_gather.13 = bf16[16,4,2048]{2,1,0:T(4,128)(2,1)S(1)} all-gather(bf16[4,4,2048]{2,1,0:T(4,128)(2,1)S(1)} %reshape.199), channel_id=1, replica_groups=mesh['groups'=2,'ctx'=4,'tp'=4] {'ctx'}, dimensions={0}, use_global_device_ids=true | all-gather | bytes 327680 | tf_op jit(solution)/shard_map/all_gather | solution.py:178
  63.8 5.9 %fusion.28 = bf16[16,4,2048]{2,0,1:T(8,128)(2,1)} fusion(bf16[2048,2048]{1,0:T(8,128)(2,1)} %param.23, bf16[16,4,2048]{2,1,0:T(4,128)(2,1)S(1)} %all_gather.13), kind=kOutput, calls=%fused_computation.40 | convolution fusion | flops 537001984 | bytes 8912896 | tf_op jit(solution)/shard_map/rte,ef->rtf/dot_general | solution.py:176
  69.7 0.2 convert_bitcast_fusion
  69.9 0.3 copy.81
  70.2 0.7 multiply_subtract_fusion
  70.9 0.8 squeeze.16
  71.7 0.6 broadcast_in_dim.104
  72.3 0.1 broadcast_in_dim.105
  72.5 1.3 %pad_maximum_fusion = bf16[192,16,128]{2,1,0:T(8,128)(2,1)} fusion(bf16[192,16,64]{2,1,0:T(8,128)(2,1)S(1)} %get-tuple-element.239, bf16[192,16,64]{2,1,0:T(8,128)(2,1)S(1)} %get-tuple-element.238), kind=kLoop, calls=%fused_computation.41 | loop fusion | flops 1572864 | bytes 1572864 | tf_op jit(solution)/shard_map/concatenate | solution.py:27
  73.8 11.0 %conditional.1 = ((f32[2,8,192]{2,1,0:T(8,128)}, f32[2,8,192,128]{3,2,1,0:T(8,128)S(1)})) conditional(s32[]{:T(128)} %convert_element_type.82, (f32[2,8,192]{2,1,0:T(8,128)}, f32[2,8,192,128]{3,2,1,0:T(8,128)S(1)}) %tuple.26, (s32[]{:T(128)}, s32[192]{0:T(256)S(1)}, bf16[192,16,128]{2,1,0:T(8,128)(2,1)}, bf16[768,2,128]{2,1,0:T(2,128)(2,1)}, ...), branch_computations={%region_0.1_spmd, %region_1.4_spmd} | conditional | flops 1239573760 | bytes 35440980 | solution.py:147
  73.8 0.2 iota_compare_fusion
  74.0 1.3 %copy.94 = bf16[192,16,128]{2,0,1:T(8,128)(2,1)S(1)} copy(bf16[192,16,128]{2,1,0:T(8,128)(2,1)} %get-tuple-element.193) | data formatting | bytes 1572864 | tf_op jit(solution)/shard_map
  75.3 2.9 %fusion = (f32[2,8,192]{2,1,0:T(8,128)S(1)}, f32[2,768,192,8]{1,2,3,0:T(8,128)S(1)}) fusion(pred[192,768]{1,0:T(8,128)(4,1)S(1)} %iota_compare_fusion, bf16[192,2,8,128]{3,0,2,1:T(8,128)(2,1)S(1)} %bitcast.126, bf16[768,2,128,1]{2,1,0,3:T(2,128)(2,1)} %bitcast.131), kind=kOutput, calls=%fused_computation.2 | convolution fusion | flops 611054592 | bytes 10776576 | tf_op jit(solution)/shard_map/while/body/eval_jaxpr/cond/branch_1_fun/qhgd,khd->hgqk/dot_general | solution.py:124
  78.2 3.1 %fusion.2 = f32[2,8,192]{2,1,0:T(8,128)S(1)} fusion(f32[2,768,192,8]{1,2,3,0:T(8,128)S(1)} %get-tuple-element.235, f32[2,8,192]{2,1,0:T(8,128)S(1)} %broadcast_maximum_fusion, pred[192,768]{1,0:T(8,128)(4,1)S(1)} %iota_compare_fusion), kind=kLoop, calls=%fused_computation.4 | loop fusion | flops 11793408 | bytes 9609216 | tf_op jit(solution)/shard_map/while/body/eval_jaxpr/cond/branch_1_fun/reduce_sum | solution.py:39
  81.3 3.5 %multiply_add_fusion = f32[2,8,192,128]{3,2,1,0:T(8,128)S(1)} fusion(f32[2,8,192,128]{3,2,1,0:T(8,128)S(1)} %get-tuple-element.110, f32[2,768,192,8]{1,2,3,0:T(8,128)S(1)} %get-tuple-element.235, f32[2,8,192]{2,1,0:T(8,128)S(1)} %broadcast_maximum_fusion, pred[192,768]{1,0:T(8,128)(4,1)S(1)} %iota_compare_fusion, f32[2,8,192]{2,1,0:T(8,128)S(1)} %get-tuple-element.232, ...), kind=kOutput, calls=%fused_computation.8 | convolution fusion | flops 616562688 | bytes 13148160 | tf_op jit(solution)/shard_map/while/body/eval_jaxpr/cond/branch_1_fun/hgqk,khd->hgqd/dot_general | solution.py:40
  84.8 1.2 %fusion.33 = bf16[192,2,8,128]{3,0,2,1:T(8,128)(2,1)S(1)} fusion(f32[2,8,192,128]{3,2,1,0:T(8,128)S(1)} %get-tuple-element.130, f32[2,8,192]{2,1,0:T(8,128)} %get-tuple-element.131), kind=kLoop, calls=%fused_computation.51 | loop fusion | flops 786432 | bytes 2371584 | tf_op jit(solution)/shard_map/transpose | solution.py:163
  86.0 0.5 copy.58
  86.5 1.1 %copy.99 = bf16[24,8,16,128]{3,1,2,0:T(8,128)(2,1)} copy(bf16[24,8,16,128]{3,2,1,0:T(8,128)(2,1)S(1)} %bitcast.125) | data formatting | bytes 1572864
  87.6 2.9 %reduce-scatter.2.cloned.1.call-done = bf16[16,4,512]{2,0,1:T(8,128)(2,1)} async-done(((bf16[16,4,2048]{2,0,1:T(8,128)(2,1)}), bf16[16,4,512]{2,0,1:T(8,128)(2,1)}) %reduce-scatter.2.cloned.1.call-update) | async-done | bytes 65552 | tf_op jit(solution)/shard_map/reduce_scatter | solution.py:182
  90.5 1.5 %copy.69 = bf16[16,4,512]{2,1,0:T(4,128)(2,1)} copy(bf16[16,4,512]{2,0,1:T(8,128)(2,1)} %reduce-scatter.2.cloned.1.call-done) | data formatting | bytes 131072
  (34 shorter events, 0.3 us)
Async XLA Ops:
  7.2 5.8 %copy-start = (bf16[4,4,256]{2,1,0:T(4,128)(2,1)S(1)}, bf16[4,4,256]{2,1,0:T(4,128)(2,1)}, u32[]{:S(2)}) copy-start(bf16[4,4,256]{2,1,0:T(4,128)(2,1)} %param.20) | copy-start | bytes 24580
  7.2 25.2 %copy-start.5 = (bf16[192,256]{1,0:T(8,128)(2,1)S(1)}, bf16[192,256]{1,0:T(8,128)(2,1)}, u32[]{:S(2)}) copy-start(bf16[192,256]{1,0:T(8,128)(2,1)} %param.16) | copy-start | bytes 294916
  7.2 83.3 %reduce-scatter.2.cloned.1.call-start = ((), (), s32[]{:S(2)}) async-start(), calls=%async_computation.1 | async-start | bytes 327680 | tf_op jit(solution)/shard_map/reduce_scatter | solution.py:182
  15.4 0.6 copy-start.2
  63.8 5.9 %copy-start.1 = (bf16[192,2048]{1,0:T(8,128)(2,1)S(1)}, bf16[192,2048]{1,0:T(8,128)(2,1)}, u32[]{:S(2)}) copy-start(bf16[192,2048]{1,0:T(8,128)(2,1)} %param.14) | copy-start | bytes 2359300
  78.2 3.1 %copy-start.3 = (f32[2,8,192]{2,1,0:T(8,128)S(1)}, f32[2,8,192]{2,1,0:T(8,128)}, u32[]{:S(2)}) copy-start(f32[2,8,192]{2,1,0:T(8,128)} %get-tuple-element.105) | copy-start | bytes 36868 | tf_op jit(solution)/shard_map/while/body/eval_jaxpr/cond
  81.3 3.5 %copy-start.4 = (f32[2,8,192]{2,1,0:T(8,128)}, f32[2,8,192]{2,1,0:T(8,128)S(1)}, u32[]{:S(2)}) copy-start(f32[2,8,192]{2,1,0:T(8,128)S(1)} %get-tuple-element.324) | copy-start | bytes 36868 | tf_op jit(solution)/shard_map/while/body/eval_jaxpr/cond
Sparse Core Ops, SparseCore 0:
  69.8 20.6 reduce-scatter.1
where the time goes:
time: 99.4 us; the launch traced here: 98.9 us
  blocking collectives  45.9 us (46%)
  between operations  15.7 us (16%)
  matrix products  13.6 us (14%)
  other arithmetic  11.2 us (11%)
  local copies, waits for them, and re-layouts  9.35 us (9%)
  waiting for transfers between devices  2.95 us (3%)
    all_gather x1, blocking collectives, local(): lax.all_gather(prompt_keys, 'ctx', axis=0, tiled=True)  16.3 us
    all_gather x1, blocking collectives, local(): lax.all_gather(prompt_v, 'ctx', axis=0, tiled=True)  15.5 us
    all_gather x1, blocking collectives, local(): lax.all_gather(attended, 'ctx', axis=0, tiled=True)  14.1 us
    dot_general x1, matrix products, local(): jnp.einsum('rte,ef->rtf', lax.all_gather(attended, 'ctx', axis=0, tiled=T...  5.87 us
    dot_general x3, matrix products, fold_scores(): jnp.einsum(form, probs.astype(jnp.bfloat16), values, preferred_element_ty...  4.1 us
    unnamed x12, local copies, waits for them, and re-layouts  3.55 us
    reduce_sum x3, other arithmetic, fold_scores(): totals = totals * decay + probs.sum(-1)  3.48 us
    reduce_scatter x1, waiting for transfers between devices, local(): lax.psum_scatter(columns.astype(jnp.bfloat16), 'tp', scatter_dimension=2,...  2.94 us
  transfers between devices with their start and end apart: 1, of which 1 were waited for; matrix products, arithmetic and copies ran while one was open for 18% of the time, Pallas kernels for 0%

commit v1 on v0

--- a/solution.py
+++ b/solution.py
@@ -1,8 +1,12 @@
+import functools
 import math
 
 import jax
 import jax.numpy as jnp
+import numpy as np
 from jax import lax
+from jax.experimental import pallas as pl
+from jax.experimental.pallas import tpu as pltpu
 from jax.sharding import PartitionSpec as P
 
 HQ = 64
@@ -95,7 +99,7 @@
     return attended.transpose(0, 3, 1, 2, 4).reshape(slot_rows, steps, kv_local * group * HD)
 
 
-def local(
+def local_general(
     prompt_q,
     prompt_k,
     prompt_v,
@@ -183,7 +187,383 @@
     return (prompt_out, prompt_keys, step_out)
 
 
+HALF = HD // 2
+LOG2E = 1.4426950408889634
+
+
+def small_powers(ctx_size, tp_size):
+    fits = [size in (2, 4, 8) for size in (ctx_size, tp_size)]
+    return all(fits)
+
+
+def frequencies():
+    exponents = np.arange(HALF, dtype=np.float32) * np.float32(-2.0 * math.log(rope_base) / HD)
+    freqs = np.exp(exponents).astype(np.float32)
+    return jnp.asarray(np.concatenate([freqs, freqs])[None, :])
+
+
+def trig_tables(positions, freqs):
+    angles = positions.astype(jnp.float32) * freqs
+    low = lax.broadcasted_iota(jnp.int32, angles.shape, 1) < HALF
+    sine = jnp.sin(angles)
+    return jnp.cos(angles), jnp.where(low, -sine, sine)
+
+
+def trig_tables_folded(start, rows, freqs):
+    half_rows = rows // 2
+    shape = (half_rows, HD)
+    low = lax.broadcasted_iota(jnp.int32, shape, 1) < HALF
+    row = lax.broadcasted_iota(jnp.int32, shape, 0)
+    positions = start + row + jnp.where(low, 0, half_rows)
+    angles = positions.astype(jnp.float32) * freqs
+    cosine = jnp.cos(angles)
+    sine = jnp.sin(angles)
+    cosine_back = pltpu.roll(cosine, HALF, 1)
+    sine_back = pltpu.roll(sine, HALF, 1)
+    cosines = jnp.concatenate(
+        [jnp.where(low, cosine, cosine_back), jnp.where(low, cosine_back, cosine)], axis=0
+    )
+    sines = jnp.concatenate(
+        [jnp.where(low, -sine, sine_back), jnp.where(low, -sine_back, sine)], axis=0
+    )
+    return cosines, sines
+
+
+def turn(values, cosines, sines):
+    wide = values.astype(jnp.float32)
+    return (wide * cosines + pltpu.roll(wide, HALF, 1) * sines).astype(jnp.bfloat16)
+
+
+def slot_lengths(lengths_ref, slot_row_ref, first, count):
+    return [lengths_ref[slot_row_ref[first + slot]] for slot in range(count)]
+
+
+def spread_rows(scalars, steps, width):
+    rows = len(scalars) * steps
+    row = lax.broadcasted_iota(jnp.int32, (rows, width), 0)
+    spread = jnp.full((rows, width), scalars[0], jnp.int32)
+    for slot in range(1, len(scalars)):
+        spread = jnp.where(row >= slot * steps, scalars[slot], spread)
+    return spread, row
+
+
+def flat_rows(ref):
+    return jnp.concatenate(
+        [ref[slot].astype(jnp.float32) for slot in range(ref.shape[0])], axis=0
+    )
+
+
+def prepare_kernel(
+    offset_ref, lengths_ref, slot_row_ref, k_ref, sq_ref, sk_ref, sv_ref, freqs_ref, keys_ref, *packs
+):
+    local_rows = k_ref.shape[0]
+    slots, steps = sq_ref.shape[:2]
+    rows = slots * steps
+    ctx_index = lax.axis_index("ctx")
+    offset = offset_ref[0]
+    freqs = freqs_ref[...]
+    cosines, sines = trig_tables_folded(offset + ctx_index * local_rows, local_rows, freqs)
+    own = slot_lengths(lengths_ref, slot_row_ref, ctx_index * slots, slots)
+    spread, row = spread_rows(own, steps, HD)
+    step_cos, step_sin = trig_tables(offset + spread + row % steps, freqs)
+    queries = flat_rows(sq_ref)
+    step_keys = flat_rows(sk_ref)
+    step_values = flat_rows(sv_ref)
+    kv_local = len(packs)
+    group = sq_ref.shape[2] // HD // kv_local
+    for g in range(kv_local):
+        span = slice(g * HD, (g + 1) * HD)
+        turned = turn(k_ref[:, span], cosines, sines)
+        keys_ref[:, span] = turned
+        packs[g][:local_rows] = turned
+        at = local_rows
+        for h in range(group):
+            lane = (g * group + h) * HD
+            packs[g][at : at + rows] = turn(queries[:, lane : lane + HD], step_cos, step_sin)
+            at += rows
+        packs[g][at : at + rows] = turn(step_keys[:, span], step_cos, step_sin)
+        packs[g][at + rows : at + 2 * rows] = step_values[:, span].astype(jnp.bfloat16)
+
+
+def rotate_queries_kernel(offset_ref, q_ref, freqs_ref, out_ref):
+    local_rows = q_ref.shape[0]
+    start = offset_ref[0] + lax.axis_index("ctx") * local_rows
+    cosines, sines = trig_tables_folded(start, local_rows, freqs_ref[...])
+    for h in range(q_ref.shape[1] // HD):
+        span = slice(h * HD, (h + 1) * HD)
+        out_ref[:, span] = turn(q_ref[:, span], cosines, sines)
+
+
+def column_positions(shape, masks, local_rows, ctx_index):
+    column = lax.broadcasted_iota(jnp.int32, shape, 1)
+    position = column
+    for at, mask in enumerate(masks):
+        source = lax.bitwise_xor(ctx_index, jnp.int32(mask))
+        inside = column >= at * local_rows
+        position = jnp.where(inside, column + (source - at) * local_rows, position)
+    return column, position
+
+
+def softmax_apply(scores, values, scale):
+    top = jnp.max(scores, axis=1, keepdims=True)
+    probs = jnp.exp2((scores - top) * (scale * LOG2E))
+    total = jnp.sum(probs, axis=1, keepdims=True)
+    mixed = jnp.dot(probs.astype(jnp.bfloat16), values, preferred_element_type=jnp.float32)
+    return mixed / total
+
+
+def score(queries, keys):
+    return lax.dot_general(
+        queries, keys, (((1,), (1,)), ((), ())), preferred_element_type=jnp.float32
+    )
+
+
+def prompt_kernel(*refs, masks, head, group, scale, aliased):
+    count = len(masks)
+    q_ref = refs[0]
+    packs = refs[1 : 1 + count]
+    values = refs[1 + count : 1 + 2 * count]
+    out_ref = refs[1 + 2 * count + (1 if aliased else 0)]
+    local_rows = q_ref.shape[0]
+    ctx_index = lax.axis_index("ctx")
+    span = slice(head * HD, (head + 1) * HD)
+    keys_all = jnp.concatenate([pack[:local_rows] for pack in packs], axis=0)
+    values_all = jnp.concatenate([value[:, span] for value in values], axis=0)
+    shape = (local_rows, count * local_rows)
+    _, position = column_positions(shape, masks, local_rows, ctx_index)
+    mine = ctx_index * local_rows + lax.broadcasted_iota(jnp.int32, shape, 0)
+    bias = jnp.where(position <= mine, 0.0, floor_score)
+    for h in range(group):
+        lanes = slice(h * HD, (h + 1) * HD)
+        scores = score(q_ref[:, lanes], keys_all) + bias
+        out_ref[:, lanes] = softmax_apply(scores, values_all, scale).astype(jnp.bfloat16)
+
+
+def decode_kernel(*refs, masks, head, group, slots, steps, scale, blocks, first, last):
+    count = len(masks)
+    lengths_ref, slot_row_ref = refs[:2]
+    packs = refs[2 : 2 + count]
+    values = refs[2 + count : 2 + 2 * count]
+    weight_ref = refs[2 + 2 * count]
+    at = 3 + 2 * count
+    carried_ref = None
+    if not first:
+        carried_ref = refs[at]
+        at += 1
+    scratch = refs[-3:]
+    outs = refs[at:-3]
+    weights, attended, sems = scratch
+    width = weights.shape[2]
+    depth = group * HD
+    order = range(blocks)
+    tp_index = lax.axis_index("tp")
+    copies = []
+    for block in order:
+        copy = pltpu.make_async_copy(
+            weight_ref.at[pl.ds(head * depth, depth), pl.ds(block * width, width)],
+            weights.at[block],
+            sems.at[block],
+        )
+        copy.start()
+        copies.append(copy)
+    rows = slots * steps
+    local_rows = values[0].shape[0]
+    ctx_index = lax.axis_index("ctx")
+    span = slice(head * HD, (head + 1) * HD)
+    base = local_rows
+    keys_at = base + group * rows
+    vals_at = keys_at + rows
+    keys_all = jnp.concatenate(
+        [pack[:local_rows] for pack in packs] + [pack[keys_at:vals_at] for pack in packs], axis=0
+    )
+    values_all = jnp.concatenate(
+        [value[:, span] for value in values] + [pack[vals_at : vals_at + rows] for pack in packs],
+        axis=0,
+    )
+    cached = count * local_rows
+    shape = (rows, cached + count * rows)
+    column, position = column_positions(shape, masks, local_rows, ctx_index)
+    for j, mask in enumerate(masks):
+        source = lax.bitwise_xor(ctx_index, jnp.int32(mask))
+        spread, row = spread_rows(
+            slot_lengths(lengths_ref, slot_row_ref, source * slots, slots), steps, shape[1]
+        )
+        step_column = column - (cached + j * rows)
+        near = (step_column >= row - row % steps) & (step_column <= row)
+        allowed = ((column < cached) & (position < spread)) | near
+        bias = jnp.where(allowed, 0.0, floor_score)
+        scores = score(packs[j][base:keys_at], keys_all)
+        scores = (scores.reshape(group, rows, shape[1]) + bias[None]).reshape(
+            group * rows, shape[1]
+        )
+        mixed = softmax_apply(scores, values_all, scale).astype(jnp.bfloat16)
+        target = pl.ds(pl.multiple_of(source * rows, rows), rows)
+        for h in range(group):
+            attended[target, h * HD : (h + 1) * HD] = mixed[h * rows : (h + 1) * rows]
+    for copy in copies:
+        copy.wait()
+    everything = attended[...]
+    for relative in list(range(1, blocks, 2)) + list(range(0, blocks, 2)):
+        block = lax.bitwise_xor(tp_index, jnp.int32(relative))
+        product = jnp.dot(everything, weights[block], preferred_element_type=jnp.float32)
+        if not first:
+            product = product + carried_ref[relative]
+        if not last:
+            outs[0][relative] = product
+        elif relative % 2:
+            for slot in range(count * slots):
+                outs[0][relative // 2, slot] = product[slot * steps : (slot + 1) * steps].astype(
+                    jnp.bfloat16
+                )
+        else:
+            for slot in range(count * slots):
+                outs[1 + relative // 2][slot] = product[slot * steps : (slot + 1) * steps]
+
+
+def swap(value, axis, mask):
+    size = lax.axis_size(axis)
+    return lax.ppermute(value, axis, [(i, i ^ mask) for i in range(size)])
+
+
+def gather_swaps(value, axis):
+    items = [value]
+    bit = lax.axis_size(axis) // 2
+    while bit:
+        items = items + [swap(item, axis, bit) for item in items]
+        bit //= 2
+    return items
+
+
+def gather_masks(axis):
+    masks = [0]
+    bit = lax.axis_size(axis) // 2
+    while bit:
+        masks = masks + [mask | bit for mask in masks]
+        bit //= 2
+    return tuple(masks)
+
+
+def local_fast(
+    prompt_q,
+    prompt_k,
+    prompt_v,
+    stretch_offset,
+    step_q,
+    step_k,
+    step_v,
+    cache_len,
+    slot_row,
+    out_weight,
+):
+    scale = HD ** (-0.5)
+    bf16 = jnp.bfloat16
+    f32 = jnp.float32
+    local_rows = prompt_q.shape[0]
+    kv_local = prompt_k.shape[1] // HD
+    group = HQ // KVH
+    slots, steps = step_q.shape[:2]
+    rows = slots * steps
+    masks = gather_masks("ctx")
+    count = len(masks)
+    blocks = lax.axis_size("tp")
+    width = out_weight.shape[1] // blocks
+    smem = pl.BlockSpec(memory_space=pltpu.SMEM)
+    vmem = pl.BlockSpec(memory_space=pltpu.VMEM)
+    hbm = pl.BlockSpec(memory_space=pl.ANY)
+    freqs = frequencies()
+    pack_rows = local_rows + (group + 2) * rows
+
+    all_values = gather_swaps(prompt_v, "ctx")
+    prompt_keys, *own_packs = pl.pallas_call(
+        prepare_kernel,
+        out_shape=[jax.ShapeDtypeStruct(prompt_k.shape, bf16)]
+        + [jax.ShapeDtypeStruct((pack_rows, HD), bf16)] * kv_local,
+        in_specs=[smem] * 3 + [vmem] * 5,
+        out_specs=[vmem] * (1 + kv_local),
+        name="prepare",
+    )(stretch_offset, cache_len, slot_row, prompt_k, step_q, step_k, step_v, freqs)
+    all_packs = [gather_swaps(pack, "ctx") for pack in own_packs]
+    queries = pl.pallas_call(
+        rotate_queries_kernel,
+        out_shape=jax.ShapeDtypeStruct(prompt_q.shape, bf16),
+        in_specs=[smem, vmem, vmem],
+        out_specs=vmem,
+        name="rotate_queries",
+    )(stretch_offset, prompt_q, freqs)
+
+    carried = None
+    prompt_out = None
+    for g in range(kv_local):
+        first = g == 0
+        last = g == kv_local - 1
+        if last:
+            shape = (count * slots, steps, width)
+            out_shape = [jax.ShapeDtypeStruct((blocks // 2,) + shape, bf16)]
+            out_shape += [jax.ShapeDtypeStruct(shape, f32)] * (blocks // 2)
+        else:
+            out_shape = [jax.ShapeDtypeStruct((blocks, count * rows, width), f32)]
+        carried = pl.pallas_call(
+            functools.partial(
+                decode_kernel,
+                masks=masks,
+                head=g,
+                group=group,
+                slots=slots,
+                steps=steps,
+                scale=scale,
+                blocks=blocks,
+                first=first,
+                last=last,
+            ),
+            out_shape=out_shape,
+            in_specs=[smem] * 2 + [vmem] * (2 * count) + [hbm] + ([] if first else [vmem]),
+            out_specs=[vmem] * len(out_shape),
+            scratch_shapes=[
+                pltpu.VMEM((blocks, group * HD, width), bf16),
+                pltpu.VMEM((count * rows, group * HD), bf16),
+                pltpu.SemaphoreType.DMA((blocks,)),
+            ],
+            name=f"decode_{g}",
+        )(
+            cache_len,
+            slot_row,
+            *all_packs[g],
+            *all_values,
+            out_weight,
+            *([] if first else [carried[0]]),
+        )
+        half = pl.BlockSpec((local_rows, group * HD), lambda i, g=g: (0, g))
+        whole = lambda shape: pl.BlockSpec(shape, lambda i: (0, 0))
+        prompt_out = pl.pallas_call(
+            functools.partial(
+                prompt_kernel, masks=masks, head=g, group=group, scale=scale, aliased=not first
+            ),
+            grid=(1,),
+            out_shape=jax.ShapeDtypeStruct(prompt_q.shape, bf16),
+            in_specs=[half]
+            + [whole((pack_rows, HD))] * count
+            + [whole(prompt_v.shape)] * count
+            + ([] if first else [hbm]),
+            out_specs=half,
+            input_output_aliases={} if first else {1 + 2 * count: 0},
+            name=f"prompt_{g}",
+        )(queries, *all_packs[g], *all_values, *([] if first else [prompt_out]))
+
+    sent, *kept = carried
+    bit = 1
+    while bit < blocks:
+        received = swap(sent, "tp", bit)
+        kept = [value + received[at].astype(f32) for at, value in enumerate(kept)]
+        bit *= 2
+        if bit < blocks:
+            sent = jnp.stack([value.astype(bf16) for value in kept[1::2]])
+            kept = kept[0::2]
+    step_out = kept[0].astype(bf16)
+    return (prompt_out, prompt_keys, step_out)
+
+
 def solution(mesh):
+    body = local_fast if small_powers(mesh.shape["ctx"], mesh.shape["tp"]) else local_general
     in_specs = (
         P(("groups", "ctx"), "tp"),
         P(("groups", "ctx"), "tp"),
@@ -201,4 +581,4 @@
         P(("groups", "ctx"), "tp"),
         P("groups", None, ("ctx", "tp")),
     )
-    return jax.shard_map(local, mesh=mesh, in_specs=in_specs, out_specs=out_specs, check_vma=False)
+    return jax.shard_map(body, mesh=mesh, in_specs=in_specs, out_specs=out_specs, check_vma=False)

time: 99.4 us -> 58.5 us (0.59)
  blocking collectives: 45.9 us -> 0 us
  Pallas kernels: 0 us -> 26.9 us
  between operations: 15.7 us -> 1.39 us
  starting transfers between devices: 0.04 us -> 14.3 us
  matrix products: 13.6 us -> 0 us
  other arithmetic: 11.2 us -> 2.52 us
  waiting for transfers between devices: 2.95 us -> 10.5 us
  local copies, waits for them, and re-layouts: 9.35 us -> 2.48 us
    all_gather x3 -> x0, blocking collectives: 45.9 us -> none  [the longest x1 16.3 us: local(): lax.all_gather(prompt_keys, 'ctx', axis=0, tiled=True)]
    pallas_call x0 -> x6, Pallas kernels: none -> 26.9 us  [the longest x2 12.1 us: local_fast(): pl.pallas_call(functools.partial(decode_kernel, masks=masks, head=g, grou...]
    ppermute x0 -> x11, starting transfers between devices: none -> 14.3 us  [swap(): return lax.ppermute(value, axis, [(i, i ^ mask) for i in range(size)])]
    dot_general x7 -> x0, matrix products: 13.6 us -> none  [the longest x1 5.87 us: local(): jnp.einsum('rte,ef->rtf', lax.all_gather(attended, 'ctx', axis=0, tiled=T...]
    ppermute x0 -> x11, waiting for transfers between devices: none -> 10.5 us  [swap(): return lax.ppermute(value, axis, [(i, i ^ mask) for i in range(size)])]
    reduce_sum x4 -> x0, other arithmetic: 4.34 us -> none  [the longest x3 3.48 us: fold_scores(): totals = totals * decay + probs.sum(-1)]
    reduce_scatter x1 -> x0, waiting for transfers between devices: 2.94 us -> none  [local(): lax.psum_scatter(columns.astype(jnp.bfloat16), 'tp', scatter_dimension=2,...]
    convert_element_type x2 -> x0, local copies, waits for them, and re-layouts: 1.87 us -> none  [rotate(): shaped = values.reshape(values.shape[:-1] + (heads, HD)).astype(jnp.float32)]
  transfers between devices with their start and end apart: 1 -> 11, of which waited for: 1 -> 5; matrix products, arithmetic and copies ran while one was open for 18% -> 0% of each run, Pallas kernels for 0% -> 35%
where the time goes in v1:
time: 58.5 us; the launch traced here: 58.1 us
  Pallas kernels  26.9 us (46%)
  starting transfers between devices  14.3 us (24%)
  waiting for transfers between devices  10.5 us (18%)
  other arithmetic  2.52 us (4%)
  local copies, waits for them, and re-layouts  2.48 us (4%)
  between operations  1.39 us (2%)
    ppermute x11, starting transfers between devices, swap(): return lax.ppermute(value, axis, [(i, i ^ mask) for i in range(size)])  14.3 us
    pallas_call x2, Pallas kernels, local_fast(): pl.pallas_call(functools.partial(decode_kernel, masks=masks, head=g, grou...  12.1 us
    ppermute x11, waiting for transfers between devices, swap(): return lax.ppermute(value, axis, [(i, i ^ mask) for i in range(size)])  10.5 us
    pallas_call x2, Pallas kernels, local_fast(): pl.pallas_call(functools.partial(prompt_kernel, masks=masks, head=g, grou...  10.1 us
    pallas_call x1, Pallas kernels, local_fast(): pl.pallas_call(rotate_queries_kernel, out_shape=jax.ShapeDtypeStruct(prom...  2.63 us
    unnamed x18, local copies, waits for them, and re-layouts  2.48 us
    pallas_call x1, Pallas kernels, local_fast(): pl.pallas_call(prepare_kernel, out_shape=[jax.ShapeDtypeStruct(prompt_k.s...  1.99 us
    convert_element_type x1, other arithmetic, local_fast(): step_out = kept[0].astype(bf16)  1.58 us
  transfers between devices with their start and end apart: 11, of which 5 were waited for; matrix products, arithmetic and copies ran while one was open for 0% of the time, Pallas kernels for 35%

profile of v1, /device:TPU:0, one launch (start us, length us, event | category | flops | bytes accessed | tf_op | source)
XLA Modules:
  0.0 58.1 jit_solution(11621667505599615401)
XLA Ops:
  0.6 4.1 %collective-permute-start.3 = (bf16[192,256]{1,0:T(8,128)(2,1)}, bf16[192,256]{1,0:T(8,128)(2,1)S(1)}, u32[]{:S(2)}, u32[]{:S(2)}) collective-permute-start(bf16[192,256]{1,0:T(8,128)(2,1)} %refs_6_.3), channel_id=1, source_target_pairs={{0,8},{4,12},{8,0},{12,4},{1,9},{5,13},{9,1},{13,5},{2,10},{6,14},... | collective-permute-start | bytes 294920 | tf_op jit(solution)/shard_map/ppermute | solution.py:425
  5.4 2.0 %prepare.1 = (bf16[192,256]{1,0:T(8,128)(2,1)}, bf16[352,128]{1,0:T(8,128)(2,1)}, bf16[352,128]{1,0:T(8,128)(2,1)}) custom-call(s32[1]{0:T(128)S(6)} %copy.16.offset_ref, s32[16]{0:T(128)} %refs_0_.3, s32[16]{0:T(128)} %refs_1_.3, bf16[192,256]{1,0:T(8,128)(2,1)} %k_ref.1, bf16[4,4,2048]{2,1,0:T(4,128)(2,1)} %sq_ref.1, bf16[4,4,256]{2,1,0:T(4,128)(2,1)} %sk_ref.1, ...), custom_call_target="tpu_custom_call" | custom-call | tf_op jit(solution)/shard_map/prepare/pallas_call | solution.py:477
  7.4 0.0 collective-permute-start.6
  7.4 2.9 %collective-permute-start = (bf16[352,128]{1,0:T(8,128)(2,1)}, bf16[352,128]{1,0:T(8,128)(2,1)S(1)}, u32[]{:S(2)}, u32[]{:S(2)}) collective-permute-start(bf16[352,128]{1,0:T(8,128)(2,1)} %get-tuple-element.9.refs_1_.refs_2_), channel_id=1, source_target_pairs={{0,8},{4,12},{8,0},{12,4},{1,9},{5,13},{9,1},{13,5},{2,10},{6,14},... | collective-permute-start | bytes 270344 | tf_op jit(solution)/shard_map/ppermute | solution.py:425
  10.3 1.6 %collective-permute-start.7 = (bf16[352,128]{1,0:T(8,128)(2,1)}, bf16[352,128]{1,0:T(8,128)(2,1)S(1)}, u32[]{:S(2)}, u32[]{:S(2)}) collective-permute-start(bf16[352,128]{1,0:T(8,128)(2,1)} %get-tuple-element.10.refs_1_.refs_2_), channel_id=1, source_target_pairs={{0,4},{4,0},{8,12},{12,8},{1,5},{5,1},{9,13},{13,9},{2,6},{6,2},{1... | collective-permute-start | bytes 270344 | tf_op jit(solution)/shard_map/ppermute | solution.py:425
  11.9 0.4 collective-permute-start.4
  12.4 0.0 collective-permute-done.3.refs_6_.refs_7_
  12.4 0.0 copy-start
  12.4 1.6 %collective-permute-start.5 = (bf16[192,256]{1,0:T(8,128)(2,1)S(1)}, bf16[192,256]{1,0:T(8,128)(2,1)S(1)}, u32[]{:S(2)}, u32[]{:S(2)}) collective-permute-start(bf16[192,256]{1,0:T(8,128)(2,1)S(1)} %collective-permute-done.3.refs_6_.refs_7_), channel_id=1, source_target_pairs={{0,4},{4,0},{8,12},{12,8},{1,5},{5,1},{9,13},{13,9},{2,6},{6,2},{1... | collective-permute-start | bytes 294920 | tf_op jit(solution)/shard_map/ppermute | solution.py:425
  13.9 3.6 %collective-permute-done.6.refs_2_.refs_3_ = bf16[352,128]{1,0:T(8,128)(2,1)S(1)} collective-permute-done((bf16[352,128]{1,0:T(8,128)(2,1)}, bf16[352,128]{1,0:T(8,128)(2,1)S(1)}, u32[]{:S(2)}, u32[]{:S(2)}) %collective-permute-start.6) | collective-permute-done | bytes 90144 | tf_op jit(solution)/shard_map/ppermute | solution.py:425
  17.5 0.0 copy-start.4
  17.5 0.0 collective-permute-start.8
  17.5 1.0 %collective-permute-done.refs_2_.refs_3_ = bf16[352,128]{1,0:T(8,128)(2,1)S(1)} collective-permute-done((bf16[352,128]{1,0:T(8,128)(2,1)}, bf16[352,128]{1,0:T(8,128)(2,1)S(1)}, u32[]{:S(2)}, u32[]{:S(2)}) %collective-permute-start) | collective-permute-done | bytes 90144 | tf_op jit(solution)/shard_map/ppermute | solution.py:425
  18.5 0.0 copy-start.3
  18.5 1.1 %collective-permute-start.1 = (bf16[352,128]{1,0:T(8,128)(2,1)}, bf16[352,128]{1,0:T(8,128)(2,1)S(1)}, u32[]{:S(2)}, u32[]{:S(2)}) collective-permute-start(bf16[352,128]{1,0:T(8,128)(2,1)} %get-tuple-element.9.refs_1_.refs_2_), channel_id=1, source_target_pairs={{0,4},{4,0},{8,12},{12,8},{1,5},{5,1},{9,13},{13,9},{2,6},{6,2},{1... | collective-permute-start | bytes 270344 | tf_op jit(solution)/shard_map/ppermute | solution.py:425
  19.6 0.0 collective-permute-done.7.refs_3_.refs_4_
  19.6 0.0 copy-start.5
  19.6 1.0 %collective-permute-start.2 = (bf16[352,128]{1,0:T(8,128)(2,1)S(1)}, bf16[352,128]{1,0:T(8,128)(2,1)S(1)}, u32[]{:S(2)}, u32[]{:S(2)}) collective-permute-start(bf16[352,128]{1,0:T(8,128)(2,1)S(1)} %collective-permute-done.refs_2_.refs_3_), channel_id=1, source_target_pairs={{0,4},{4,0},{8,12},{12,8},{1,5},{5,1},{9,13},{13,9},{2,6},{6,2},{1... | collective-permute-start | bytes 270344 | tf_op jit(solution)/shard_map/ppermute | solution.py:425
  20.5 0.4 collective-permute-done.4.refs_7_.refs_8_
  20.9 0.0 copy-start.1
  20.9 4.0 %collective-permute-done.8.refs_4_.refs_5_ = bf16[352,128]{1,0:T(8,128)(2,1)S(1)} collective-permute-done((bf16[352,128]{1,0:T(8,128)(2,1)S(1)}, bf16[352,128]{1,0:T(8,128)(2,1)S(1)}, u32[]{:S(2)}, u32[]{:S(2)}) %collective-permute-start.8) | collective-permute-done | bytes 90144 | tf_op jit(solution)/shard_map/ppermute | solution.py:425
  24.9 0.0 copy-start.6
  24.9 0.0 collective-permute-done.5.refs_8_.refs_9_
  24.9 0.0 copy-done
  24.9 0.0 copy-done.4
  24.9 0.0 copy-done.5
  25.0 0.0 copy-done.1
  25.0 0.6 %copy-done.6 = bf16[352,128]{1,0:T(8,128)(2,1)} copy-done((bf16[352,128]{1,0:T(8,128)(2,1)}, bf16[352,128]{1,0:T(8,128)(2,1)S(1)}, u32[]{:S(2)}) %copy-start.6) | copy-done | bytes 90136
  25.6 0.0 copy-start.2
  25.6 0.6 %copy-done.2 = bf16[192,256]{1,0:T(8,128)(2,1)} copy-done((bf16[192,256]{1,0:T(8,128)(2,1)}, bf16[192,256]{1,0:T(8,128)(2,1)S(1)}, u32[]{:S(2)}) %copy-start.2) | copy-done | bytes 98328
  26.2 5.9 %decode_0.1.refs_11_ = f32[4,64,512]{2,1,0:T(8,128)} custom-call(s32[16]{0:T(128)} %refs_0_.3, s32[16]{0:T(128)} %refs_1_.3, bf16[352,128]{1,0:T(8,128)(2,1)} %get-tuple-element.10.refs_1_.refs_2_, bf16[352,128]{1,0:T(8,128)(2,1)} %copy-done.4, bf16[352,128]{1,0:T(8,128)(2,1)} %copy-done.5, bf16[352,128]{1,0:T(8,128)(2,1)} %copy-done.6, ...), custom_call_target="tpu_custom_call" | custom-call | tf_op jit(solution)/shard_map/decode_0/pallas_call | solution.py:505
  32.1 0.0 collective-permute-done.1.refs_3_.refs_4_
  32.1 0.0 copy-start.7
  32.1 0.0 collective-permute-done.2.refs_4_.refs_5_
  32.1 0.0 copy-done.3
  32.1 0.6 %copy-done.7 = bf16[352,128]{1,0:T(8,128)(2,1)} copy-done((bf16[352,128]{1,0:T(8,128)(2,1)}, bf16[352,128]{1,0:T(8,128)(2,1)S(1)}, u32[]{:S(2)}) %copy-start.7) | copy-done | bytes 90136
  32.7 0.0 copy-start.8
  32.7 0.6 %copy-done.8 = bf16[352,128]{1,0:T(8,128)(2,1)} copy-done((bf16[352,128]{1,0:T(8,128)(2,1)}, bf16[352,128]{1,0:T(8,128)(2,1)S(1)}, u32[]{:S(2)}) %copy-start.8) | copy-done | bytes 90136
  33.3 6.3 %decode_1.1 = (bf16[2,16,4,512]{3,2,1,0:T(4,128)(2,1)}, f32[16,4,512]{2,1,0:T(4,128)}, f32[16,4,512]{2,1,0:T(4,128)}) custom-call(s32[16]{0:T(128)} %refs_0_.3, s32[16]{0:T(128)} %refs_1_.3, bf16[352,128]{1,0:T(8,128)(2,1)} %get-tuple-element.9.refs_1_.refs_2_, bf16[352,128]{1,0:T(8,128)(2,1)} %copy-done.3, bf16[352,128]{1,0:T(8,128)(2,1)} %copy-done.7, ...), custom_call_target="tpu_custom_call" | custom-call | tf_op jit(solution)/shard_map/decode_1/pallas_call | solution.py:505
  39.6 0.1 collective-permute-start.9
  39.7 1.5 %collective-permute-done.9 = bf16[2,16,4,512]{3,2,1,0:T(4,128)(2,1)S(1)} collective-permute-done((bf16[2,16,4,512]{3,2,1,0:T(4,128)(2,1)}, bf16[2,16,4,512]{3,2,1,0:T(4,128)(2,1)S(1)}, u32[]{:S(2)}, u32[]{:S(2)}) %collective-permute-start.9) | collective-permute-done | bytes 131104 | tf_op jit(solution)/shard_map/ppermute | solution.py:425
  41.2 0.9 %fusion.2 = bf16[1,16,4,512]{3,2,1,0:T(4,128)(2,1)S(1)} fusion(f32[16,4,512]{2,1,0:T(4,128)} %get-tuple-element.14, bf16[2,16,4,512]{3,2,1,0:T(4,128)(2,1)S(1)} %collective-permute-done.9), kind=kLoop, calls=%fused_computation.5 | loop fusion | flops 98304 | bytes 262144 | tf_op jit(solution)/shard_map/stack | solution.py:559
  42.2 1.6 %collective-permute-start.10 = (bf16[1,16,4,512]{3,2,1,0:T(4,128)(2,1)S(1)}, bf16[1,16,4,512]{3,2,1,0:T(4,128)(2,1)S(1)}, u32[]{:S(2)}, u32[]{:S(2)}) collective-permute-start(bf16[1,16,4,512]{3,2,1,0:T(4,128)(2,1)S(1)} %fusion.2), channel_id=1, source_target_pairs={{0,2},{1,3},{2,0},{3,1},{4,6},{5,7},{6,4},{7,5},{8,10},{9,11},{10,... | collective-permute-start | bytes 196616 | tf_op jit(solution)/shard_map/ppermute | solution.py:425
  43.7 2.6 %rotate_queries.1.refs_0_ = bf16[192,2048]{1,0:T(8,128)(2,1)} custom-call(s32[1]{0:T(128)S(6)} %copy.16.offset_ref, bf16[192,2048]{1,0:T(8,128)(2,1)} %q_ref.1, f32[1,128]{1,0:T(1,128)} %constant.2.clone.freqs_ref), custom_call_target="tpu_custom_call" | custom-call | tf_op jit(solution)/shard_map/rotate_queries/pallas_call | solution.py:486
  46.4 5.1 %prompt_0.1.refs_9_ = bf16[192,2048]{1,0:T(8,128)(2,1)} custom-call(bf16[192,2048]{1,0:T(8,128)(2,1)} %rotate_queries.1.refs_0_, bf16[352,128]{1,0:T(8,128)(2,1)} %get-tuple-element.10.refs_1_.refs_2_, bf16[352,128]{1,0:T(8,128)(2,1)} %copy-done.4, bf16[352,128]{1,0:T(8,128)(2,1)} %copy-done.5, bf16[352,128]{1,0:T(8,128)(2,1)} %copy-done.6, ...), custom_call_target="tpu_custom_call" | custom-call | tf_op jit(solution)/shard_map/prompt_0/pallas_call | solution.py:537
  51.4 5.1 %prompt_1.1 = bf16[192,2048]{1,0:T(8,128)(2,1)} custom-call(bf16[192,2048]{1,0:T(8,128)(2,1)} %rotate_queries.1.refs_0_, bf16[352,128]{1,0:T(8,128)(2,1)} %get-tuple-element.9.refs_1_.refs_2_, bf16[352,128]{1,0:T(8,128)(2,1)} %copy-done.3, bf16[352,128]{1,0:T(8,128)(2,1)} %copy-done.7, bf16[352,128]{1,0:T(8,128)(2,1)} %copy-done.8, ...), custom_call_target="tpu_custom_call", output_to_operand_aliasing={{}: (9, {})} | custom-call | tf_op jit(solution)/shard_map/prompt_1/pallas_call | solution.py:537
  56.5 0.0 collective-permute-done.10
  56.5 1.6 %fusion = bf16[16,4,512]{2,1,0:T(4,128)(2,1)} fusion(f32[16,4,512]{2,1,0:T(4,128)} %get-tuple-element.12, bf16[2,16,4,512]{3,2,1,0:T(4,128)(2,1)S(1)} %collective-permute-done.9, bf16[1,16,4,512]{3,2,1,0:T(4,128)(2,1)S(1)} %collective-permute-done.10), kind=kLoop, calls=%fused_computation.1 | loop fusion | flops 163840 | bytes 327680 | tf_op jit(solution)/shard_map/convert_element_type | solution.py:561
Async XLA Ops:
  0.6 11.7 %collective-permute-start.3 = (bf16[192,256]{1,0:T(8,128)(2,1)}, bf16[192,256]{1,0:T(8,128)(2,1)S(1)}, u32[]{:S(2)}, u32[]{:S(2)}) collective-permute-start(bf16[192,256]{1,0:T(8,128)(2,1)} %refs_6_.3), channel_id=1, source_target_pairs={{0,8},{4,12},{8,0},{12,4},{1,9},{5,13},{9,1},{13,5},{2,10},{6,14},... | collective-permute-start | bytes 294920 | tf_op jit(solution)/shard_map/ppermute | solution.py:425
  7.4 10.1 %collective-permute-start.6 = (bf16[352,128]{1,0:T(8,128)(2,1)}, bf16[352,128]{1,0:T(8,128)(2,1)S(1)}, u32[]{:S(2)}, u32[]{:S(2)}) collective-permute-start(bf16[352,128]{1,0:T(8,128)(2,1)} %get-tuple-element.10.refs_1_.refs_2_), channel_id=1, source_target_pairs={{0,8},{4,12},{8,0},{12,4},{1,9},{5,13},{9,1},{13,5},{2,10},{6,14},... | collective-permute-start | bytes 270344 | tf_op jit(solution)/shard_map/ppermute | solution.py:425
  7.4 11.1 %collective-permute-start = (bf16[352,128]{1,0:T(8,128)(2,1)}, bf16[352,128]{1,0:T(8,128)(2,1)S(1)}, u32[]{:S(2)}, u32[]{:S(2)}) collective-permute-start(bf16[352,128]{1,0:T(8,128)(2,1)} %get-tuple-element.9.refs_1_.refs_2_), channel_id=1, source_target_pairs={{0,8},{4,12},{8,0},{12,4},{1,9},{5,13},{9,1},{13,5},{2,10},{6,14},... | collective-permute-start | bytes 270344 | tf_op jit(solution)/shard_map/ppermute | solution.py:425
  10.3 9.2 %collective-permute-start.7 = (bf16[352,128]{1,0:T(8,128)(2,1)}, bf16[352,128]{1,0:T(8,128)(2,1)S(1)}, u32[]{:S(2)}, u32[]{:S(2)}) collective-permute-start(bf16[352,128]{1,0:T(8,128)(2,1)} %get-tuple-element.10.refs_1_.refs_2_), channel_id=1, source_target_pairs={{0,4},{4,0},{8,12},{12,8},{1,5},{5,1},{9,13},{13,9},{2,6},{6,2},{1... | collective-permute-start | bytes 270344 | tf_op jit(solution)/shard_map/ppermute | solution.py:425
  11.9 9.0 %collective-permute-start.4 = (bf16[192,256]{1,0:T(8,128)(2,1)}, bf16[192,256]{1,0:T(8,128)(2,1)S(1)}, u32[]{:S(2)}, u32[]{:S(2)}) collective-permute-start(bf16[192,256]{1,0:T(8,128)(2,1)} %refs_6_.3), channel_id=1, source_target_pairs={{0,4},{4,0},{8,12},{12,8},{1,5},{5,1},{9,13},{13,9},{2,6},{6,2},{1... | collective-permute-start | bytes 294920 | tf_op jit(solution)/shard_map/ppermute | solution.py:425
  12.4 12.6 %copy-start = (bf16[192,256]{1,0:T(8,128)(2,1)}, bf16[192,256]{1,0:T(8,128)(2,1)S(1)}, u32[]{:S(2)}) copy-start(bf16[192,256]{1,0:T(8,128)(2,1)S(1)} %collective-permute-done.3.refs_6_.refs_7_) | copy-start | bytes 294916
  12.4 12.6 %collective-permute-start.5 = (bf16[192,256]{1,0:T(8,128)(2,1)S(1)}, bf16[192,256]{1,0:T(8,128)(2,1)S(1)}, u32[]{:S(2)}, u32[]{:S(2)}) collective-permute-start(bf16[192,256]{1,0:T(8,128)(2,1)S(1)} %collective-permute-done.3.refs_6_.refs_7_), channel_id=1, source_target_pairs={{0,4},{4,0},{8,12},{12,8},{1,5},{5,1},{9,13},{13,9},{2,6},{6,2},{1... | collective-permute-start | bytes 294920 | tf_op jit(solution)/shard_map/ppermute | solution.py:425
  17.5 7.4 %copy-start.4 = (bf16[352,128]{1,0:T(8,128)(2,1)}, bf16[352,128]{1,0:T(8,128)(2,1)S(1)}, u32[]{:S(2)}) copy-start(bf16[352,128]{1,0:T(8,128)(2,1)S(1)} %collective-permute-done.6.refs_2_.refs_3_) | copy-start | bytes 270340
  17.5 7.4 %collective-permute-start.8 = (bf16[352,128]{1,0:T(8,128)(2,1)S(1)}, bf16[352,128]{1,0:T(8,128)(2,1)S(1)}, u32[]{:S(2)}, u32[]{:S(2)}) collective-permute-start(bf16[352,128]{1,0:T(8,128)(2,1)S(1)} %collective-permute-done.6.refs_2_.refs_3_), channel_id=1, source_target_pairs={{0,4},{4,0},{8,12},{12,8},{1,5},{5,1},{9,13},{13,9},{2,6},{6,2},{1... | collective-permute-start | bytes 270344 | tf_op jit(solution)/shard_map/ppermute | solution.py:425
  18.5 13.6 %copy-start.3 = (bf16[352,128]{1,0:T(8,128)(2,1)}, bf16[352,128]{1,0:T(8,128)(2,1)S(1)}, u32[]{:S(2)}) copy-start(bf16[352,128]{1,0:T(8,128)(2,1)S(1)} %collective-permute-done.refs_2_.refs_3_) | copy-start | bytes 270340
  18.5 13.6 %collective-permute-start.1 = (bf16[352,128]{1,0:T(8,128)(2,1)}, bf16[352,128]{1,0:T(8,128)(2,1)S(1)}, u32[]{:S(2)}, u32[]{:S(2)}) collective-permute-start(bf16[352,128]{1,0:T(8,128)(2,1)} %get-tuple-element.9.refs_1_.refs_2_), channel_id=1, source_target_pairs={{0,4},{4,0},{8,12},{12,8},{1,5},{5,1},{9,13},{13,9},{2,6},{6,2},{1... | collective-permute-start | bytes 270344 | tf_op jit(solution)/shard_map/ppermute | solution.py:425
  19.6 5.4 %copy-start.5 = (bf16[352,128]{1,0:T(8,128)(2,1)}, bf16[352,128]{1,0:T(8,128)(2,1)S(1)}, u32[]{:S(2)}) copy-start(bf16[352,128]{1,0:T(8,128)(2,1)S(1)} %collective-permute-done.7.refs_3_.refs_4_) | copy-start | bytes 270340
  19.6 12.5 %collective-permute-start.2 = (bf16[352,128]{1,0:T(8,128)(2,1)S(1)}, bf16[352,128]{1,0:T(8,128)(2,1)S(1)}, u32[]{:S(2)}, u32[]{:S(2)}) collective-permute-start(bf16[352,128]{1,0:T(8,128)(2,1)S(1)} %collective-permute-done.refs_2_.refs_3_), channel_id=1, source_target_pairs={{0,4},{4,0},{8,12},{12,8},{1,5},{5,1},{9,13},{13,9},{2,6},{6,2},{1... | collective-permute-start | bytes 270344 | tf_op jit(solution)/shard_map/ppermute | solution.py:425
  20.9 4.1 %copy-start.1 = (bf16[192,256]{1,0:T(8,128)(2,1)}, bf16[192,256]{1,0:T(8,128)(2,1)S(1)}, u32[]{:S(2)}) copy-start(bf16[192,256]{1,0:T(8,128)(2,1)S(1)} %collective-permute-done.4.refs_7_.refs_8_) | copy-start | bytes 294916
  24.9 0.6 %copy-start.6 = (bf16[352,128]{1,0:T(8,128)(2,1)}, bf16[352,128]{1,0:T(8,128)(2,1)S(1)}, u32[]{:S(2)}) copy-start(bf16[352,128]{1,0:T(8,128)(2,1)S(1)} %collective-permute-done.8.refs_4_.refs_5_) | copy-start | bytes 270340
  25.6 0.6 %copy-start.2 = (bf16[192,256]{1,0:T(8,128)(2,1)}, bf16[192,256]{1,0:T(8,128)(2,1)S(1)}, u32[]{:S(2)}) copy-start(bf16[192,256]{1,0:T(8,128)(2,1)S(1)} %collective-permute-done.5.refs_8_.refs_9_) | copy-start | bytes 294916
  32.1 0.6 %copy-start.7 = (bf16[352,128]{1,0:T(8,128)(2,1)}, bf16[352,128]{1,0:T(8,128)(2,1)S(1)}, u32[]{:S(2)}) copy-start(bf16[352,128]{1,0:T(8,128)(2,1)S(1)} %collective-permute-done.1.refs_3_.refs_4_) | copy-start | bytes 270340
  32.7 0.6 %copy-start.8 = (bf16[352,128]{1,0:T(8,128)(2,1)}, bf16[352,128]{1,0:T(8,128)(2,1)S(1)}, u32[]{:S(2)}) copy-start(bf16[352,128]{1,0:T(8,128)(2,1)S(1)} %collective-permute-done.2.refs_4_.refs_5_) | copy-start | bytes 270340
  39.6 1.6 %collective-permute-start.9 = (bf16[2,16,4,512]{3,2,1,0:T(4,128)(2,1)}, bf16[2,16,4,512]{3,2,1,0:T(4,128)(2,1)S(1)}, u32[]{:S(2)}, u32[]{:S(2)}) collective-permute-start(bf16[2,16,4,512]{3,2,1,0:T(4,128)(2,1)} %get-tuple-element.13), channel_id=1, source_target_pairs={{0,1},{1,0},{2,3},{3,2},{4,5},{5,4},{6,7},{7,6},{8,9},{9,8},{10,11... | collective-permute-start | bytes 393224 | tf_op jit(solution)/shard_map/ppermute | solution.py:425
  42.2 14.3 %collective-permute-start.10 = (bf16[1,16,4,512]{3,2,1,0:T(4,128)(2,1)S(1)}, bf16[1,16,4,512]{3,2,1,0:T(4,128)(2,1)S(1)}, u32[]{:S(2)}, u32[]{:S(2)}) collective-permute-start(bf16[1,16,4,512]{3,2,1,0:T(4,128)(2,1)S(1)} %fusion.2), channel_id=1, source_target_pairs={{0,2},{1,3},{2,0},{3,1},{4,6},{5,7},{6,4},{7,5},{8,10},{9,11},{10,... | collective-permute-start | bytes 196616 | tf_op jit(solution)/shard_map/ppermute | solution.py:425
